TPU v7x, 256 devices: a whole 4x4x8 slice. The times are simulated.
256 devices in a mesh: freq: 8 (over y, x_hi), rec: 32 (over x_lo, z, core).
Axes of the slice: x: 4 (x_hi: 2, x_lo: 2; x = x_hi * 2 + x_lo), y: 4, z: 8, core: 2. Of those that a mesh axis runs over, the one named last changes fastest.
Arguments:
- response: bfloat16 [128, 2, 1792, 1792], P('freq', None, 'rec'), may hold values from -1 to 1, as said below
- direct: float32 [1792, 32, 256], P('rec', 'freq'), may hold values from -6 to 6
- onset: int32 [1792, 32], P('rec', 'freq'), may hold values from 16 to 128
Outputs:
- upgoing: float32 [1792, 32, 256], P('rec', 'freq')
- coda: float32 [1792, 32, 256], P('rec', 'freq')
Inputs may be any that keep to these rules, and one draw needn't show every extreme that they name: response[k, c, r, s] = response[k, c, s, r] for every frequency and part (source-receiver reciprocity).
All inputs are finite; a program needn't handle non-finite values.
Results may differ from a plain program's by a relative error of at most 0.023.
Values may be sent and summed in bfloat16 or wider, within the bound.
A program may use at most 128 MiB of HBM per device.

v0:
```python
import math
import jax
import jax.numpy as jnp
from jax import lax
from jax.sharding import PartitionSpec as P

NF = 128
NT = 256
ITERS = 2


def spectral_tables(length, count):
    samples = jnp.arange(length, dtype=jnp.int32)
    frequency_bins = jnp.arange(1, count + 1, dtype=jnp.int32)
    phase = (samples[:, None] * frequency_bins[None, :] % length).astype(jnp.float32) * (
        2.0 * math.pi / length
    )
    cosine = jnp.cos(phase)
    sine = jnp.sin(phase)
    forward = jnp.stack([cosine, -sine], axis=1)
    inverse = jnp.stack([cosine.T, -sine.T], axis=0) * (2.0 / length)
    return (forward, inverse)


def make_window(onset, length):
    samples = jnp.arange(length, dtype=jnp.int32)
    folded = jnp.minimum(samples, length - samples)
    return (folded[None, None, :] < onset[:, :, None]).astype(jnp.float32)


def to_spectrum(field, forward):
    packed = jnp.einsum("svt,tck->kcvs", field, forward)
    return packed.astype(jnp.bfloat16)


def to_time(spectra, inverse):
    return jnp.einsum("kcvs,ckt->svt", spectra.astype(jnp.float32), inverse)


def complex_apply(block, spectra, conj_sign):
    parts = jnp.einsum("fcrs,fdvs->cdfvr", block, spectra, preferred_element_type=jnp.float32)
    real_out = parts[0, 0] - conj_sign * parts[1, 1]
    imag_out = parts[0, 1] + conj_sign * parts[1, 0]
    return jnp.stack([real_out, imag_out], axis=1)


def body(response, direct, onset):
    forward, inverse = spectral_tables(NT, NF)
    window = make_window(onset, NT)
    coda = jnp.zeros_like(direct)
    upgoing = coda
    for iteration in range(ITERS):
        downgoing = direct + coda
        sources = lax.all_to_all(
            to_spectrum(downgoing, forward), "freq", split_axis=0, concat_axis=2, tiled=True
        )
        gathered = lax.all_gather(sources, "rec", axis=3, tiled=True)
        reflected = complex_apply(response, gathered, 1.0)
        reflected_time = lax.all_to_all(
            reflected.astype(jnp.bfloat16), "freq", split_axis=2, concat_axis=0, tiled=True
        )
        upgoing = window * to_time(reflected_time, inverse)
        spectra_up = lax.all_to_all(
            to_spectrum(upgoing, forward), "freq", split_axis=0, concat_axis=2, tiled=True
        )
        receivers = lax.all_gather(spectra_up, "rec", axis=3, tiled=True)
        returned = complex_apply(response, receivers, -1.0)
        returned_time = lax.all_to_all(
            returned.astype(jnp.bfloat16), "freq", split_axis=2, concat_axis=0, tiled=True
        )
        coda = window * to_time(returned_time, inverse)
    return (upgoing, coda)


def solution(mesh):
    placed = (P("freq", None, "rec", None), P("rec", "freq", None), P("rec", "freq"))
    return jax.shard_map(
        body,
        mesh=mesh,
        in_specs=placed,
        out_specs=(P("rec", "freq", None), P("rec", "freq", None)),
        check_vma=False,
    )
```

profile of v0, /device:TPU:96, one launch (start us, length us, event | category | flops | bytes accessed | tf_op | source)
XLA Modules:
  0.0 545.7 jit_solution(14085154062390279766)
XLA Ops:
  7.2 0.5 fusion.96
  7.8 1.1 fusion.39
  8.9 0.2 copy.86
  9.1 0.4 reshape.396
  9.5 14.9 %all_to_all.144 = bf16[8,2,3584]{2,1,0:T(2,128)(2,1)S(1)} all-to-all(bf16[8,2,3584]{2,1,0:T(2,128)(2,1)S(1)} %reshape.396), channel_id=1, replica_groups=mesh['freq'=8,'rec'=32] {'freq'}, dimensions={0} | all-to-all | bytes 229376 | tf_op jit(solution)/shard_map/all_to_all | solution.py:54
  24.4 0.4 reshape.397
  24.9 1.5 copy.89
  26.4 0.6 fusion.97
  27.0 87.4 %all-gather.5.cloned.1.call-done = bf16[16,2,32,1792]{2,0,1,3:T(8,128)(2,1)} async-done(((bf16[16,2,32,56]{2,0,1,3:T(8,128)(2,1)}), bf16[16,2,32,1792]{2,0,1,3:T(8,128)(2,1)}) %all-gather.5.cloned.1.call-update) | async-done | bytes 3670032 | tf_op jit(solution)/shard_map/all_gather | solution.py:57
  114.4 15.0 %fusion.17 = f32[2,2,16,32,56]{4,3,0,1,2:T(8,128)S(1)} fusion(bf16[16,2,56,1792]{3,2,1,0:T(8,128)(2,1)} %param.3, bf16[16,2,32,1792,1]{2,0,1,3,4:T(8,128)(2,1)} %bitcast.271), kind=kOutput, calls=%fused_computation.13 | convolution fusion | flops 411041792 | bytes 10551296 | tf_op jit(solution)/shard_map/fcrs,fdvs->cdfvr/dot_general | solution.py:41
  129.5 0.1 fusion.77
  129.6 0.1 pad_maximum_fusion
  129.6 0.1 copy.198
  129.7 1.1 reshape.398
  130.8 6.7 %all-to-all-start.1 = ((bf16[8,2,3584]{2,1,0:T(2,128)(2,1)}), bf16[8,2,3584]{2,1,0:T(2,128)(2,1)S(1)}, u32[]{:S(2)}, u32[]{:S(2)}) async-start(bf16[8,2,3584]{2,1,0:T(2,128)(2,1)} %reshape.398), calls=%async_computation.1 | async-start | bytes 229376 | tf_op jit(solution)/shard_map/all_to_all | solution.py:59
  137.6 8.1 %all-to-all-done.1 = bf16[8,2,3584]{2,1,0:T(2,128)(2,1)S(1)} async-done(((bf16[8,2,3584]{2,1,0:T(2,128)(2,1)}), bf16[8,2,3584]{2,1,0:T(2,128)(2,1)S(1)}, u32[]{:S(2)}, u32[]{:S(2)}) %all-to-all-start.1) | async-done | bytes 114720 | tf_op jit(solution)/shard_map/all_to_all | solution.py:59
  145.6 0.4 reshape.399
  146.1 0.4 fusion.40
  146.5 0.2 copy.96
  146.7 0.4 reshape.400
  147.1 10.5 %all_to_all.145 = bf16[8,2,3584]{2,1,0:T(2,128)(2,1)S(1)} all-to-all(bf16[8,2,3584]{2,1,0:T(2,128)(2,1)S(1)} %reshape.400), channel_id=1, replica_groups=mesh['freq'=8,'rec'=32] {'freq'}, dimensions={0} | all-to-all | bytes 229376 | tf_op jit(solution)/shard_map/all_to_all | solution.py:63
  157.6 0.4 reshape.401
  158.2 1.5 copy.99
  159.6 0.2 all-gather.9.cloned.1.call-start
  159.9 85.8 %all-gather.7.cloned.1.call-done = bf16[16,2,32,1792]{2,0,1,3:T(8,128)(2,1)} async-done(((bf16[16,2,32,56]{2,0,1,3:T(8,128)(2,1)}), bf16[16,2,32,1792]{2,0,1,3:T(8,128)(2,1)}) %all-gather.7.cloned.1.call-update) | async-done | bytes 3670032 | tf_op jit(solution)/shard_map/all_gather | solution.py:66
  245.6 15.1 %fusion.22 = f32[2,2,16,32,56]{4,3,0,1,2:T(8,128)S(1)} fusion(bf16[16,2,56,1792]{3,2,1,0:T(8,128)(2,1)} %param.3, bf16[16,2,32,1792,1]{2,0,1,3,4:T(8,128)(2,1)} %bitcast.272), kind=kOutput, calls=%fused_computation.14 | convolution fusion | flops 411041792 | bytes 10551296 | tf_op jit(solution)/shard_map/fcrs,fdvs->cdfvr/dot_general | solution.py:41
  260.7 0.1 fusion.79
  260.9 0.1 copy.197
  261.0 0.4 reshape.402
  261.4 14.6 %all_to_all.146 = bf16[8,2,3584]{2,1,0:T(2,128)(2,1)S(1)} all-to-all(bf16[8,2,3584]{2,1,0:T(2,128)(2,1)S(1)} %reshape.402), channel_id=1, replica_groups=mesh['freq'=8,'rec'=32] {'freq'}, dimensions={0} | all-to-all | bytes 229376 | tf_op jit(solution)/shard_map/all_to_all | solution.py:68
  276.1 0.4 reshape.403
  276.5 0.4 fusion.41
  276.9 0.2 copy.108
  277.1 0.4 reshape.404
  277.5 10.5 %all_to_all.147 = bf16[8,2,3584]{2,1,0:T(2,128)(2,1)S(1)} all-to-all(bf16[8,2,3584]{2,1,0:T(2,128)(2,1)S(1)} %reshape.404), channel_id=1, replica_groups=mesh['freq'=8,'rec'=32] {'freq'}, dimensions={0} | all-to-all | bytes 229376 | tf_op jit(solution)/shard_map/all_to_all | solution.py:54
  288.1 0.4 reshape.405
  288.6 1.5 copy.111
  290.1 0.3 all-gather.11.cloned.1.call-start
  290.3 85.7 %all-gather.9.cloned.1.call-done = bf16[16,2,32,1792]{2,0,1,3:T(8,128)(2,1)} async-done(((bf16[16,2,32,56]{2,0,1,3:T(8,128)(2,1)}), bf16[16,2,32,1792]{2,0,1,3:T(8,128)(2,1)}) %all-gather.9.cloned.1.call-update) | async-done | bytes 3670032 | tf_op jit(solution)/shard_map/all_gather | solution.py:57
  376.0 15.0 %fusion.27 = f32[2,2,16,32,56]{4,3,0,1,2:T(8,128)S(1)} fusion(bf16[16,2,56,1792]{3,2,1,0:T(8,128)(2,1)} %param.3, bf16[16,2,32,1792,1]{2,0,1,3,4:T(8,128)(2,1)} %bitcast.273), kind=kOutput, calls=%fused_computation.15 | convolution fusion | flops 411041792 | bytes 10551296 | tf_op jit(solution)/shard_map/fcrs,fdvs->cdfvr/dot_general | solution.py:41
  391.1 0.1 fusion.81
  391.2 0.1 copy.196
  391.3 0.4 reshape.406
  391.8 14.6 %all_to_all.148 = bf16[8,2,3584]{2,1,0:T(2,128)(2,1)S(1)} all-to-all(bf16[8,2,3584]{2,1,0:T(2,128)(2,1)S(1)} %reshape.406), channel_id=1, replica_groups=mesh['freq'=8,'rec'=32] {'freq'}, dimensions={0} | all-to-all | bytes 229376 | tf_op jit(solution)/shard_map/all_to_all | solution.py:59
  406.4 0.4 reshape.407
  406.9 0.2 fusion.37
  407.1 0.2 fusion.42
  407.3 0.2 copy.118
  407.5 0.4 reshape.408
  407.9 10.5 %all_to_all.149 = bf16[8,2,3584]{2,1,0:T(2,128)(2,1)S(1)} all-to-all(bf16[8,2,3584]{2,1,0:T(2,128)(2,1)S(1)} %reshape.408), channel_id=1, replica_groups=mesh['freq'=8,'rec'=32] {'freq'}, dimensions={0} | all-to-all | bytes 229376 | tf_op jit(solution)/shard_map/all_to_all | solution.py:63
  418.5 0.4 reshape.409
  419.0 1.5 copy.121
  420.5 86.0 %all-gather.11.cloned.1.call-done = bf16[16,2,32,1792]{2,0,1,3:T(8,128)(2,1)} async-done(((bf16[16,2,32,56]{2,0,1,3:T(8,128)(2,1)}), bf16[16,2,32,1792]{2,0,1,3:T(8,128)(2,1)}) %all-gather.11.cloned.1.call-update) | async-done | bytes 3670032 | tf_op jit(solution)/shard_map/all_gather | solution.py:66
  506.5 15.0 %fusion.12 = f32[2,2,16,32,56]{4,3,2,1,0:T(8,128)S(1)} fusion(bf16[16,2,32,1792,1]{2,0,1,3,4:T(8,128)(2,1)} %bitcast.274, bf16[16,2,56,1792]{3,2,1,0:T(8,128)(2,1)} %param.3), kind=kOutput, calls=%fused_computation.12 | convolution fusion | flops 411041792 | bytes 10551296 | tf_op jit(solution)/shard_map/fcrs,fdvs->cdfvr/dot_general | solution.py:41
  521.5 0.1 fusion.82
  521.6 0.1 pad_maximum_fusion.3
  521.7 0.1 copy.195
  521.8 1.1 reshape.410
  522.8 6.7 %all-to-all-start.7 = ((bf16[8,2,3584]{2,1,0:T(2,128)(2,1)}), bf16[8,2,3584]{2,1,0:T(2,128)(2,1)S(1)}, u32[]{:S(2)}, u32[]{:S(2)}) async-start(bf16[8,2,3584]{2,1,0:T(2,128)(2,1)} %reshape.410), calls=%async_computation.7 | async-start | bytes 229376 | tf_op jit(solution)/shard_map/all_to_all | solution.py:68
  529.5 0.8 copy.127
  530.3 7.4 %all-to-all-done.7 = bf16[8,2,3584]{2,1,0:T(2,128)(2,1)S(1)} async-done(((bf16[8,2,3584]{2,1,0:T(2,128)(2,1)}), bf16[8,2,3584]{2,1,0:T(2,128)(2,1)S(1)}, u32[]{:S(2)}, u32[]{:S(2)}) %all-to-all-start.7) | async-done | bytes 114720 | tf_op jit(solution)/shard_map/all_to_all | solution.py:68
  537.7 0.4 reshape.411
  538.2 0.2 fusion.38
  538.4 0.8 copy.128
  (29 shorter events, 0.7 us)
Async XLA Ops:
  7.2 107.3 %all-gather.5.cloned.1.call-start = ((), (), s32[]{:S(2)}) async-start(), calls=%async_computation.8 | async-start | bytes 15138816 | tf_op jit(solution)/shard_map/all_gather | solution.py:57
  114.4 31.7 %copy-start.1 = (s32[56,4]{0,1:T(4,128)S(1)}, s32[56,4]{0,1:T(4,128)}, u32[]{:S(2)}) copy-start(s32[56,4]{0,1:T(4,128)} %param.5) | copy-start | bytes 2692
  130.8 14.8 %all-to-all-start.1 = ((bf16[8,2,3584]{2,1,0:T(2,128)(2,1)}), bf16[8,2,3584]{2,1,0:T(2,128)(2,1)S(1)}, u32[]{:S(2)}, u32[]{:S(2)}) async-start(bf16[8,2,3584]{2,1,0:T(2,128)(2,1)} %reshape.398), calls=%async_computation.1 | async-start | bytes 229376 | tf_op jit(solution)/shard_map/all_to_all | solution.py:59
  137.5 108.1 %all-gather.7.cloned.1.call-start = ((), (), s32[]{:S(2)}) async-start(), calls=%async_computation.9 | async-start | bytes 15138816 | tf_op jit(solution)/shard_map/all_gather | solution.py:66
  159.6 216.4 %all-gather.9.cloned.1.call-start = ((), (), s32[]{:S(2)}) async-start(), calls=%async_computation.10 | async-start | bytes 15138816 | tf_op jit(solution)/shard_map/all_gather | solution.py:57
  245.6 30.9 %copy-start = (f32[56,4,256]{2,1,0:T(4,128)S(1)}, f32[56,4,256]{2,1,0:T(4,128)}, u32[]{:S(2)}) copy-start(f32[56,4,256]{2,1,0:T(4,128)} %param.4) | copy-start | bytes 688132
  290.1 216.4 %all-gather.11.cloned.1.call-start = ((), (), s32[]{:S(2)}) async-start(), calls=%async_computation.11 | async-start | bytes 15138816 | tf_op jit(solution)/shard_map/all_gather | solution.py:66
  522.8 14.8 %all-to-all-start.7 = ((bf16[8,2,3584]{2,1,0:T(2,128)(2,1)}), bf16[8,2,3584]{2,1,0:T(2,128)(2,1)S(1)}, u32[]{:S(2)}, u32[]{:S(2)}) async-start(bf16[8,2,3584]{2,1,0:T(2,128)(2,1)} %reshape.410), calls=%async_computation.7 | async-start | bytes 229376 | tf_op jit(solution)/shard_map/all_to_all | solution.py:68
Sparse Core Ops, SparseCore 0:
  26.5 87.8 all-gather.4
  159.8 85.8 all-gather.6
  290.2 85.8 all-gather.8
  420.6 85.8 all-gather.10
where the time goes:
time: 546 us
  waiting for transfers between devices  360 us (66%)
  blocking collectives  75.7 us (14%)
  matrix products  62.6 us (11%)
  local copies, waits for them, and re-layouts  17 us (3%)
  between operations  14.2 us (3%)
  starting transfers between devices  14 us (3%)
    all_gather x2, waiting for transfers between devices, body(): gathered = lax.all_gather(sources, 'rec', axis=3, tiled=True)  173 us
    all_gather x2, waiting for transfers between devices, body(): receivers = lax.all_gather(spectra_up, 'rec', axis=3, tiled=True)  172 us
    dot_general x4, matrix products, complex_apply(): jnp.einsum('fcrs,fdvs->cdfvr', block, spectra, preferred_element_type=jnp...  60.1 us
    all_to_all x2, blocking collectives, body(): lax.all_to_all(to_spectrum(downgoing, forward), 'freq', split_axis=0, con...  25.4 us
    all_to_all x2, blocking collectives, body(): lax.all_to_all(to_spectrum(upgoing, forward), 'freq', split_axis=0, conca...  21.1 us
    all_to_all x1, blocking collectives, body(): lax.all_to_all(reflected.astype(jnp.bfloat16), 'freq', split_axis=2, conc...  14.6 us
    all_to_all x1, blocking collectives, body(): lax.all_to_all(returned.astype(jnp.bfloat16), 'freq', split_axis=2, conca...  14.6 us
  transfers between devices with their start and end apart: 6, of which 6 were waited for; matrix products, arithmetic and copies ran while one was open for 0% of the time, Pallas kernels for 0%

commit v1 on v0

--- a/solution.py
+++ b/solution.py
@@ -65,9 +65,11 @@
         )
         receivers = lax.all_gather(spectra_up, "rec", axis=3, tiled=True)
         returned = complex_apply(response, receivers, -1.0)
-        returned_time = lax.all_to_all(
-            returned.astype(jnp.bfloat16), "freq", split_axis=2, concat_axis=0, tiled=True
-        )
+        own = returned.astype(jnp.bfloat16)
+        size = lax.axis_size("freq")
+        pieces = jnp.stack(jnp.split(own, size, axis=2), axis=0)
+        pieces = lax.all_to_all(pieces, "freq", split_axis=0, concat_axis=0)
+        returned_time = jnp.concatenate(pieces, axis=0)
         coda = window * to_time(returned_time, inverse)
     return (upgoing, coda)
 

time: 546 us -> 547 us (level)
  no operation moved by 1% of the time
where the time goes in v1:
time: 547 us; the launch traced here: 546 us
  waiting for transfers between devices  360 us (66%)
  blocking collectives  75.7 us (14%)
  matrix products  62.7 us (11%)
  local copies, waits for them, and re-layouts  16.8 us (3%)
  between operations  14.2 us (3%)
  starting transfers between devices  14 us (3%)
    all_gather x2, waiting for transfers between devices, body(): gathered = lax.all_gather(sources, 'rec', axis=3, tiled=True)  173 us
    all_gather x2, waiting for transfers between devices, body(): receivers = lax.all_gather(spectra_up, 'rec', axis=3, tiled=True)  172 us
    dot_general x4, matrix products, complex_apply(): jnp.einsum('fcrs,fdvs->cdfvr', block, spectra, preferred_element_type=jnp...  60.1 us
    all_to_all x2, blocking collectives, body(): lax.all_to_all(to_spectrum(downgoing, forward), 'freq', split_axis=0, con...  25.4 us
    all_to_all x2, blocking collectives, body(): lax.all_to_all(to_spectrum(upgoing, forward), 'freq', split_axis=0, conca...  21.1 us
    all_to_all x1, blocking collectives, body(): lax.all_to_all(reflected.astype(jnp.bfloat16), 'freq', split_axis=2, conc...  14.6 us
    all_to_all x1, blocking collectives, body(): pieces = lax.all_to_all(pieces, 'freq', split_axis=0, concat_axis=0)  14.6 us
  transfers between devices with their start and end apart: 6, of which 6 were waited for; matrix products, arithmetic and copies ran while one was open for 0% of the time, Pallas kernels for 0%

profile of v1, /device:TPU:96, one launch (start us, length us, event | category | flops | bytes accessed | tf_op | source)
XLA Modules:
  0.0 546.0 jit_solution(10637572400658094554)
XLA Ops:
  7.2 0.0 all-gather.5.cloned.1.call-start
  7.2 0.5 fusion.96
  7.8 1.1 fusion.39
  8.9 0.2 copy.83
  9.1 0.4 reshape.404
  9.5 14.9 %all_to_all.118 = bf16[8,2,3584]{2,1,0:T(2,128)(2,1)S(1)} all-to-all(bf16[8,2,3584]{2,1,0:T(2,128)(2,1)S(1)} %reshape.404), channel_id=1, replica_groups=mesh['freq'=8,'rec'=32] {'freq'}, dimensions={0} | all-to-all | bytes 229376 | tf_op jit(solution)/shard_map/all_to_all | solution.py:54
  24.4 0.4 reshape.405
  24.9 1.5 copy.86
  26.4 0.6 fusion.97
  27.0 87.4 %all-gather.5.cloned.1.call-done = bf16[16,2,32,1792]{2,0,1,3:T(8,128)(2,1)} async-done(((bf16[16,2,32,56]{2,0,1,3:T(8,128)(2,1)}), bf16[16,2,32,1792]{2,0,1,3:T(8,128)(2,1)}) %all-gather.5.cloned.1.call-update) | async-done | bytes 3670032 | tf_op jit(solution)/shard_map/all_gather | solution.py:57
  114.4 15.0 %fusion.17 = f32[2,2,16,32,56]{4,3,0,1,2:T(8,128)S(1)} fusion(bf16[16,2,56,1792]{3,2,1,0:T(8,128)(2,1)} %param.3, bf16[16,2,32,1792,1]{2,0,1,3,4:T(8,128)(2,1)} %bitcast.293), kind=kOutput, calls=%fused_computation.13 | convolution fusion | flops 411041792 | bytes 10551296 | tf_op jit(solution)/shard_map/fcrs,fdvs->cdfvr/dot_general | solution.py:41
  129.5 0.1 fusion.77
  129.6 0.1 pad_maximum_fusion
  129.6 0.1 copy.191
  129.7 1.1 reshape.406
  130.8 6.7 %all-to-all-start.1 = ((bf16[8,2,3584]{2,1,0:T(2,128)(2,1)}), bf16[8,2,3584]{2,1,0:T(2,128)(2,1)S(1)}, u32[]{:S(2)}, u32[]{:S(2)}) async-start(bf16[8,2,3584]{2,1,0:T(2,128)(2,1)} %reshape.406), calls=%async_computation.1 | async-start | bytes 229376 | tf_op jit(solution)/shard_map/all_to_all | solution.py:59
  137.5 0.0 all-gather.7.cloned.1.call-start
  137.6 8.1 %all-to-all-done.1 = bf16[8,2,3584]{2,1,0:T(2,128)(2,1)S(1)} async-done(((bf16[8,2,3584]{2,1,0:T(2,128)(2,1)}), bf16[8,2,3584]{2,1,0:T(2,128)(2,1)S(1)}, u32[]{:S(2)}, u32[]{:S(2)}) %all-to-all-start.1) | async-done | bytes 114720 | tf_op jit(solution)/shard_map/all_to_all | solution.py:59
  145.7 0.4 reshape.407
  146.1 0.4 fusion.40
  146.5 0.2 copy.93
  146.7 0.4 reshape.408
  147.1 10.5 %all_to_all.119 = bf16[8,2,3584]{2,1,0:T(2,128)(2,1)S(1)} all-to-all(bf16[8,2,3584]{2,1,0:T(2,128)(2,1)S(1)} %reshape.408), channel_id=1, replica_groups=mesh['freq'=8,'rec'=32] {'freq'}, dimensions={0} | all-to-all | bytes 229376 | tf_op jit(solution)/shard_map/all_to_all | solution.py:63
  157.7 0.4 reshape.409
  158.2 1.5 copy.96
  159.7 0.2 all-gather.9.cloned.1.call-start
  159.9 85.8 %all-gather.7.cloned.1.call-done = bf16[16,2,32,1792]{2,0,1,3:T(8,128)(2,1)} async-done(((bf16[16,2,32,56]{2,0,1,3:T(8,128)(2,1)}), bf16[16,2,32,1792]{2,0,1,3:T(8,128)(2,1)}) %all-gather.7.cloned.1.call-update) | async-done | bytes 3670032 | tf_op jit(solution)/shard_map/all_gather | solution.py:66
  245.7 15.1 %fusion.22 = f32[2,2,16,32,56]{4,3,0,1,2:T(8,128)S(1)} fusion(bf16[16,2,56,1792]{3,2,1,0:T(8,128)(2,1)} %param.3, bf16[16,2,32,1792,1]{2,0,1,3,4:T(8,128)(2,1)} %bitcast.294), kind=kOutput, calls=%fused_computation.14 | convolution fusion | flops 411041792 | bytes 10551296 | tf_op jit(solution)/shard_map/fcrs,fdvs->cdfvr/dot_general | solution.py:41
  260.7 0.1 fusion.79
  261.1 0.4 reshape.410
  261.5 14.6 %all_to_all.120 = bf16[8,2,3584]{2,1,0:T(2,128)(2,1)S(1)} all-to-all(bf16[8,2,3584]{2,1,0:T(2,128)(2,1)S(1)} %reshape.410), channel_id=1, replica_groups=mesh['freq'=8,'rec'=32] {'freq'}, dimensions={0} | all-to-all | bytes 229376 | tf_op jit(solution)/shard_map/all_to_all | solution.py:71
  276.2 0.4 reshape.411
  276.7 0.4 fusion.41
  277.0 0.2 copy.104
  277.2 0.4 reshape.412
  277.6 10.5 %all_to_all.121 = bf16[8,2,3584]{2,1,0:T(2,128)(2,1)S(1)} all-to-all(bf16[8,2,3584]{2,1,0:T(2,128)(2,1)S(1)} %reshape.412), channel_id=1, replica_groups=mesh['freq'=8,'rec'=32] {'freq'}, dimensions={0} | all-to-all | bytes 229376 | tf_op jit(solution)/shard_map/all_to_all | solution.py:54
  288.2 0.4 reshape.413
  288.7 1.5 copy.107
  290.2 0.3 all-gather.11.cloned.1.call-start
  290.4 85.7 %all-gather.9.cloned.1.call-done = bf16[16,2,32,1792]{2,0,1,3:T(8,128)(2,1)} async-done(((bf16[16,2,32,56]{2,0,1,3:T(8,128)(2,1)}), bf16[16,2,32,1792]{2,0,1,3:T(8,128)(2,1)}) %all-gather.9.cloned.1.call-update) | async-done | bytes 3670032 | tf_op jit(solution)/shard_map/all_gather | solution.py:57
  376.2 15.0 %fusion.27 = f32[2,2,16,32,56]{4,3,0,1,2:T(8,128)S(1)} fusion(bf16[16,2,56,1792]{3,2,1,0:T(8,128)(2,1)} %param.3, bf16[16,2,32,1792,1]{2,0,1,3,4:T(8,128)(2,1)} %bitcast.295), kind=kOutput, calls=%fused_computation.15 | convolution fusion | flops 411041792 | bytes 10551296 | tf_op jit(solution)/shard_map/fcrs,fdvs->cdfvr/dot_general | solution.py:41
  391.2 0.1 fusion.81
  391.3 0.1 pad_maximum_fusion.1
  391.4 0.1 copy.190
  391.5 0.4 reshape.414
  391.9 14.6 %all_to_all.122 = bf16[8,2,3584]{2,1,0:T(2,128)(2,1)S(1)} all-to-all(bf16[8,2,3584]{2,1,0:T(2,128)(2,1)S(1)} %reshape.414), channel_id=1, replica_groups=mesh['freq'=8,'rec'=32] {'freq'}, dimensions={0} | all-to-all | bytes 229376 | tf_op jit(solution)/shard_map/all_to_all | solution.py:59
  406.5 0.4 reshape.415
  407.0 0.2 fusion.38
  407.3 0.2 fusion.42
  407.4 0.2 copy.114
  407.6 0.4 reshape.416
  408.1 10.5 %all_to_all.123 = bf16[8,2,3584]{2,1,0:T(2,128)(2,1)S(1)} all-to-all(bf16[8,2,3584]{2,1,0:T(2,128)(2,1)S(1)} %reshape.416), channel_id=1, replica_groups=mesh['freq'=8,'rec'=32] {'freq'}, dimensions={0} | all-to-all | bytes 229376 | tf_op jit(solution)/shard_map/all_to_all | solution.py:63
  418.6 0.4 reshape.417
  419.1 1.5 copy.117
  420.6 86.0 %all-gather.11.cloned.1.call-done = bf16[16,2,32,1792]{2,0,1,3:T(8,128)(2,1)} async-done(((bf16[16,2,32,56]{2,0,1,3:T(8,128)(2,1)}), bf16[16,2,32,1792]{2,0,1,3:T(8,128)(2,1)}) %all-gather.11.cloned.1.call-update) | async-done | bytes 3670032 | tf_op jit(solution)/shard_map/all_gather | solution.py:66
  506.6 15.0 %fusion.12 = f32[2,2,16,32,56]{4,3,2,1,0:T(8,128)S(1)} fusion(bf16[16,2,32,1792,1]{2,0,1,3,4:T(8,128)(2,1)} %bitcast.296, bf16[16,2,56,1792]{3,2,1,0:T(8,128)(2,1)} %param.3), kind=kOutput, calls=%fused_computation.12 | convolution fusion | flops 411041792 | bytes 10551296 | tf_op jit(solution)/shard_map/fcrs,fdvs->cdfvr/dot_general | solution.py:41
  521.6 0.1 fusion.82
  522.0 1.1 reshape.418
  523.1 6.7 %all-to-all-start.7 = ((bf16[8,2,3584]{2,1,0:T(2,128)(2,1)}), bf16[8,2,3584]{2,1,0:T(2,128)(2,1)S(1)}, u32[]{:S(2)}, u32[]{:S(2)}) async-start(bf16[8,2,3584]{2,1,0:T(2,128)(2,1)} %reshape.418), calls=%async_computation.7 | async-start | bytes 229376 | tf_op jit(solution)/shard_map/all_to_all | solution.py:71
  529.8 0.8 copy.122
  530.5 7.4 %all-to-all-done.7 = bf16[8,2,3584]{2,1,0:T(2,128)(2,1)S(1)} async-done(((bf16[8,2,3584]{2,1,0:T(2,128)(2,1)}), bf16[8,2,3584]{2,1,0:T(2,128)(2,1)S(1)}, u32[]{:S(2)}, u32[]{:S(2)}) %all-to-all-start.7) | async-done | bytes 114720 | tf_op jit(solution)/shard_map/all_to_all | solution.py:71
  537.9 0.4 reshape.419
  538.4 0.2 fusion.35
  538.6 0.8 copy.123
  (41 shorter events, 1.0 us)
Async XLA Ops:
  7.2 107.3 %all-gather.5.cloned.1.call-start = ((), (), s32[]{:S(2)}) async-start(), calls=%async_computation.8 | async-start | bytes 15138816 | tf_op jit(solution)/shard_map/all_gather | solution.py:57
  114.4 31.7 %copy-start = (s32[56,4]{0,1:T(4,128)S(1)}, s32[56,4]{0,1:T(4,128)}, u32[]{:S(2)}) copy-start(s32[56,4]{0,1:T(4,128)} %param.5) | copy-start | bytes 2692
  130.8 14.8 %all-to-all-start.1 = ((bf16[8,2,3584]{2,1,0:T(2,128)(2,1)}), bf16[8,2,3584]{2,1,0:T(2,128)(2,1)S(1)}, u32[]{:S(2)}, u32[]{:S(2)}) async-start(bf16[8,2,3584]{2,1,0:T(2,128)(2,1)} %reshape.406), calls=%async_computation.1 | async-start | bytes 229376 | tf_op jit(solution)/shard_map/all_to_all | solution.py:59
  137.5 108.1 %all-gather.7.cloned.1.call-start = ((), (), s32[]{:S(2)}) async-start(), calls=%async_computation.9 | async-start | bytes 15138816 | tf_op jit(solution)/shard_map/all_gather | solution.py:66
  159.7 216.5 %all-gather.9.cloned.1.call-start = ((), (), s32[]{:S(2)}) async-start(), calls=%async_computation.10 | async-start | bytes 15138816 | tf_op jit(solution)/shard_map/all_gather | solution.py:57
  245.7 31.0 %copy-start.1 = (f32[56,4,256]{2,1,0:T(4,128)S(1)}, f32[56,4,256]{2,1,0:T(4,128)}, u32[]{:S(2)}) copy-start(f32[56,4,256]{2,1,0:T(4,128)} %param.4) | copy-start | bytes 688132
  290.2 216.4 %all-gather.11.cloned.1.call-start = ((), (), s32[]{:S(2)}) async-start(), calls=%async_computation.11 | async-start | bytes 15138816 | tf_op jit(solution)/shard_map/all_gather | solution.py:66
  523.1 14.8 %all-to-all-start.7 = ((bf16[8,2,3584]{2,1,0:T(2,128)(2,1)}), bf16[8,2,3584]{2,1,0:T(2,128)(2,1)S(1)}, u32[]{:S(2)}, u32[]{:S(2)}) async-start(bf16[8,2,3584]{2,1,0:T(2,128)(2,1)} %reshape.418), calls=%async_computation.7 | async-start | bytes 229376 | tf_op jit(solution)/shard_map/all_to_all | solution.py:71
Sparse Core Ops, SparseCore 0:
  26.5 87.8 all-gather.4
  159.8 85.8 all-gather.6
  290.3 85.8 all-gather.8
  420.7 85.8 all-gather.10
